TPU v7x, 32 devices: a whole 2x2x4 slice. The times are simulated.
32 devices in a mesh: tm: 8 (over z, x), chan: 4 (over y, core).
Axes of the slice: x: 2, y: 2, z: 4, core: 2. Of those that a mesh axis runs over, the one named last changes fastest.
Arguments:
- surveillance: bfloat16 [128, 1024, 256], P(('chan', 'tm')), parts along dimension 0, may hold values from -6 to 6
- ref_samples: bfloat16 [32, 1040, 256], P('tm'), may hold values from -6 to 6
- block_ids: int32 [32], P('tm'), may hold values from 0 to 31, each once
- walk: int32 [32], P('tm'), may hold values from 0 to 63
- cfar_guard: int32 [2048], P('tm'), may hold values from 1 to 8
- cfar_window: int32 [2048], P('tm'), may hold values from 1 to 16
Outputs:
- detection: float32 [8192, 512], P(('chan', 'tm')), parts along dimension 0
There are 4 independent parts, one for each index of `chan`. A program takes and returns all parts, laid end to end along the dimension named above; an argument that names none is the same for every part. Nothing has to cross between parts.
Inputs may be any that keep to these rules, and one draw needn't show every extreme that they name: block_ids names each of 0 to 31 exactly once.
All inputs are finite; a program needn't handle non-finite values.
Results may differ from a plain program's by a relative error of at most 0.0003.
Values sent between devices are 32-bit elements; how exact they have to be, the bound alone decides.
No kernel may reach another device: no remote copies, remote signals or barrier semaphores. Data moves between devices by JAX's collectives and lax.ppermute only.
A program may use at most 64 MiB of HBM per device.

v0:
```python
import math
import jax
import jax.numpy as jnp
from jax import lax
from jax.sharding import PartitionSpec as P

D = 2048
DOP = 512
SEGS = 64
GUARD_MAX = 8
WIN_MAX = 16
HIGH = lax.Precision.HIGHEST


def with_halo(x, sides, width):
    for axis, dim in sides:
        count, length = (lax.axis_size(axis), x.shape[dim])
        up = [(i, (i + 1) % count) for i in range(count - 1)]
        down = [(j, i) for i, j in up]
        last = lax.slice_in_dim(x, length - width, length, axis=dim)
        initial = lax.slice_in_dim(x, 0, width, axis=dim)
        before = lax.ppermute(last, axis, up)
        after = lax.ppermute(initial, axis, down)
        x = jnp.concatenate([before, x, after], axis=dim)
    return x


def phase(product, total):
    return 2.0 * math.pi / total * (product % total).astype(jnp.float32)


def square_tables(width):
    place = jnp.arange(width, dtype=jnp.int32)
    theta = phase(place[:, None] * place[None, :], width)
    return (jnp.cos(theta), jnp.sin(theta))


def make_tables():
    length = 2 * D
    rows = length // 128
    small_cos, small_sin = square_tables(rows)
    wide_cos, wide_sin = square_tables(128)
    mixer = jnp.concatenate(
        [jnp.concatenate([wide_cos, -wide_sin], 1), jnp.concatenate([wide_sin, wide_cos], 1)], 0
    )
    first_idx = jnp.arange(rows, dtype=jnp.int32)[:, None]
    second_idx = jnp.arange(128, dtype=jnp.int32)[None, :]
    twist = phase(first_idx * second_idx, length)
    spread = first_idx + rows * second_idx
    return (small_cos, small_sin, jnp.cos(twist), jnp.sin(twist), mixer, spread)


def forward(signal, tables):
    small_cos, small_sin, twist_cos, twist_sin, mixer, spread = tables
    first = jnp.einsum("kn,snc->skc", small_cos, signal, precision=HIGH)
    second = jnp.einsum("kn,snc->skc", small_sin, signal, precision=HIGH)
    real_part = first[..., :128] + second[..., 128:]
    imag_part = first[..., 128:] - second[..., :128]
    turned = jnp.concatenate(
        [
            real_part * twist_cos + imag_part * twist_sin,
            imag_part * twist_cos - real_part * twist_sin,
        ],
        axis=-1,
    )
    return jnp.einsum("skc,cd->skd", turned, mixer, precision=HIGH)


def inverse(spectrum, tables):
    small_cos, small_sin, twist_cos, twist_sin, mixer, spread = tables
    mixed = jnp.dot(spectrum, mixer.T, precision=HIGH)
    real_part = mixed[:, :128]
    imag_part = mixed[:, 128:]
    turned = jnp.concatenate(
        [
            real_part * twist_cos - imag_part * twist_sin,
            imag_part * twist_cos + real_part * twist_sin,
        ],
        axis=-1,
    )
    with_cos = jnp.dot(small_cos, turned, precision=HIGH)
    with_sin = jnp.dot(small_sin, turned, precision=HIGH)
    result = jnp.concatenate(
        [with_cos[:, :128] - with_sin[:, 128:], with_cos[:, 128:] + with_sin[:, :128]], axis=-1
    )
    return result / (2.0 * D)


def correlate(surv_rows, ref_rows, shift, tables):
    seg_rows = D // 128
    rows_all = surv_rows.shape[0]
    segs = rows_all // seg_rows
    echo = surv_rows.astype(jnp.float32).reshape(segs, seg_rows, 256)
    echo = jnp.concatenate([echo, jnp.zeros_like(echo)], axis=1)
    direct = ref_rows.astype(jnp.float32)
    direct = jnp.concatenate(
        [
            direct[:rows_all].reshape(segs, seg_rows, 256),
            direct[seg_rows:].reshape(segs, seg_rows, 256),
        ],
        axis=1,
    )
    echo_hat = forward(echo, tables)
    direct_hat = forward(direct, tables)
    echo_re = echo_hat[..., :128]
    echo_im = echo_hat[..., 128:]
    direct_re = direct_hat[..., :128]
    direct_im = direct_hat[..., 128:]
    spec_re = jnp.sum(echo_re * direct_re + echo_im * direct_im, axis=0)
    spec_im = jnp.sum(echo_im * direct_re - echo_re * direct_im, axis=0)
    ramp = phase(tables[5] * shift, 2 * D)
    ramp_cos = jnp.cos(ramp)
    ramp_sin = jnp.sin(ramp)
    turned = jnp.concatenate(
        [spec_re * ramp_cos + spec_im * ramp_sin, spec_im * ramp_cos - spec_re * ramp_sin], axis=-1
    )
    lagged = inverse(turned, tables)
    picked = lagged[seg_rows:]
    delay_idx = (
        128 * jnp.arange(seg_rows, dtype=jnp.int32)[:, None]
        + (jnp.arange(256, dtype=jnp.int32) % 128)[None, :]
    )
    return jnp.where(delay_idx >= shift, picked, 0.0)


def doppler_mixer(ids, norm):
    freq = jnp.arange(DOP, dtype=jnp.int32)
    theta = phase(ids[:, None] * freq[None, :], DOP)
    cos_table = jnp.cos(theta) * norm
    sin_table = jnp.sin(theta) * norm
    return jnp.concatenate(
        [jnp.concatenate([cos_table, -sin_table], 1), jnp.concatenate([sin_table, cos_table], 1)], 0
    )


def body(surveillance, ref_samples, block_ids, walk, cfar_guard, cfar_window):
    blocks = surveillance.shape[0]
    devices = lax.axis_size("tm")
    total_blocks = blocks * devices
    span = D // devices
    reach = GUARD_MAX + WIN_MAX
    base = lax.axis_index("tm") * span
    tables = make_tables()
    corr = lax.map(
        lambda item: correlate(item[0], item[1], item[2], tables), (surveillance, ref_samples, walk)
    )
    real_c = corr[:, :, :128].reshape(blocks, D)
    imag_c = corr[:, :, 128:].reshape(blocks, D)
    norm = 1.0 / math.sqrt(total_blocks * SEGS * D)
    moved = lax.all_to_all(
        jnp.stack([real_c, imag_c], axis=1), "tm", split_axis=2, concat_axis=0, tiled=True
    )
    ids = lax.all_gather(block_ids, "tm", axis=0, tiled=True)
    stacked = jnp.concatenate([moved[:, 0], moved[:, 1]], 0)
    mixer = doppler_mixer(ids, norm)
    amp = lax.dot_general(stacked, mixer, (((0,), (0,)), ((), ())), precision=HIGH)
    floor = jnp.sum(moved * moved, axis=(0, 1))
    floor = floor / (total_blocks * SEGS * D)
    power = amp[:, :DOP] * amp[:, :DOP] + amp[:, DOP:] * amp[:, DOP:]
    padded = with_halo(power, (("tm", 0),), reach)
    guard = cfar_guard[:, None]
    width = cfar_window[:, None]

    def inside(dist):
        return ((dist > guard) & (dist <= guard + width)).astype(jnp.float32)

    row_idx = jnp.arange(span, dtype=jnp.int32)[:, None]
    col_idx = jnp.arange(span + 2 * reach, dtype=jnp.int32)[None, :]
    band = inside(jnp.abs(col_idx - reach - row_idx))
    spot = base + jnp.arange(span + 2 * reach, dtype=jnp.int32) - reach
    valid = ((spot >= 0) & (spot < D)).astype(jnp.float32)
    delay_sum = jnp.dot(band, padded, precision=HIGH)
    count = jnp.dot(band, valid, precision=HIGH)
    doppler_sum = jnp.zeros_like(power)
    for step in range(1, reach + 1):
        active = inside(jnp.full((1, 1), step, jnp.int32))
        doppler_sum = doppler_sum + active * (
            jnp.roll(power, -step, axis=1) + jnp.roll(power, step, axis=1)
        )
    noise = (delay_sum + doppler_sum) / (count[:, None] + 2.0 * width.astype(jnp.float32))
    return (power - floor[:, None]) / (0.25 + noise)


def solution(mesh):
    in_specs = (
        P(("chan", "tm"), None, None),
        P("tm", None, None),
        P("tm"),
        P("tm"),
        P("tm"),
        P("tm"),
    )
    out_specs = P(("chan", "tm"), None)
    return jax.shard_map(body, mesh=mesh, in_specs=in_specs, out_specs=out_specs, check_vma=False)
```

profile of v0, /device:TPU:0, one launch (start us, length us, event | category | flops | bytes accessed | tf_op | source)
XLA Modules:
  0.0 126.7 jit_solution(17962002947929078072)
XLA Ops:
  0.6 69.0 %while.15 = (s32[]{:T(128)}, f32[4,16,256]{2,1,0:T(8,128)S(1)}, s32[4]{0:T(128)}, bf16[4,1024,256]{2,1,0:T(8,128)(2,1)}, f32[256,256]{1,0:T(8,128)S(1)}, /*index...) while((s32[]{:T(128)}, f32[4,16,256]{2,1,0:T(8,128)S(1)}, s32[4]{0:T(128)}, ...), condition=%wide.region_3.4_spmd.clone.clone, body=%wide.region_0.3_spmd.clone.clone.sunk | while | flops 4067001856 | bytes 47000764 | solution.py:144
  4.4 2.0 %fusion.285 = f32[64,32,256]{2,1,0:T(8,128)S(1)} fusion(f32[64,16,256]{2,1,0:T(8,128)S(1)} %bitcast.89, f32[64,16,256]{2,1,0:T(8,128)S(1)} %bitcast.87), kind=kOutput, calls=%fused_computation.16.clone.1 | convolution fusion | flops 201865216 | bytes 4194304 | tf_op jit(solution)/shard_map/while/body/eval_jaxpr/kn,snc->skc/dot_general | solution.py:55
  6.4 2.0 %fusion.284 = f32[64,32,256]{2,1,0:T(8,128)S(1)} fusion(f32[64,16,256]{2,1,0:T(8,128)S(1)} %bitcast.90, f32[64,16,256]{2,1,0:T(8,128)S(1)} %bitcast.88), kind=kOutput, calls=%fused_computation.17.clone.1 | convolution fusion | flops 201865216 | bytes 4194304 | tf_op jit(solution)/shard_map/while/body/eval_jaxpr/kn,snc->skc/dot_general | solution.py:56
  11.3 1.9 %fusion.286 = f32[64,32,256]{2,1,0:T(8,128)S(1)} fusion(f32[64,32,128]{2,1,0:T(8,128)S(1)} %get-tuple-element.512, f32[64,32,128]{2,1,0:T(8,128)S(1)} %get-tuple-element.513, f32[256,256]{1,0:T(8,128)S(1)} %get-tuple-element.544), kind=kOutput, calls=%fused_computation.10.clone.1 | convolution fusion | flops 1611137024 | bytes 4456448 | tf_op jit(solution)/shard_map/while/body/eval_jaxpr/skc,cd->skd/dot_general | solution.py:66
  13.2 1.9 %fusion.287 = f32[64,32,256]{2,1,0:T(8,128)S(1)} fusion(f32[64,32,128]{2,1,0:T(8,128)S(1)} %get-tuple-element.514, f32[64,32,128]{2,1,0:T(8,128)S(1)} %get-tuple-element.515, f32[256,256]{1,0:T(8,128)S(1)} %get-tuple-element.544), kind=kOutput, calls=%fused_computation.5.clone.1 | convolution fusion | flops 1611137024 | bytes 4456448 | tf_op jit(solution)/shard_map/while/body/eval_jaxpr/skc,cd->skd/dot_general | solution.py:66
  21.6 2.0 %fusion.285 = f32[64,32,256]{2,1,0:T(8,128)S(1)} fusion(f32[64,16,256]{2,1,0:T(8,128)S(1)} %bitcast.89, f32[64,16,256]{2,1,0:T(8,128)S(1)} %bitcast.87), kind=kOutput, calls=%fused_computation.16.clone.1 | convolution fusion | flops 201865216 | bytes 4194304 | tf_op jit(solution)/shard_map/while/body/eval_jaxpr/kn,snc->skc/dot_general | solution.py:55
  23.6 2.0 %fusion.284 = f32[64,32,256]{2,1,0:T(8,128)S(1)} fusion(f32[64,16,256]{2,1,0:T(8,128)S(1)} %bitcast.90, f32[64,16,256]{2,1,0:T(8,128)S(1)} %bitcast.88), kind=kOutput, calls=%fused_computation.17.clone.1 | convolution fusion | flops 201865216 | bytes 4194304 | tf_op jit(solution)/shard_map/while/body/eval_jaxpr/kn,snc->skc/dot_general | solution.py:56
  28.5 1.9 %fusion.286 = f32[64,32,256]{2,1,0:T(8,128)S(1)} fusion(f32[64,32,128]{2,1,0:T(8,128)S(1)} %get-tuple-element.512, f32[64,32,128]{2,1,0:T(8,128)S(1)} %get-tuple-element.513, f32[256,256]{1,0:T(8,128)S(1)} %get-tuple-element.544), kind=kOutput, calls=%fused_computation.10.clone.1 | convolution fusion | flops 1611137024 | bytes 4456448 | tf_op jit(solution)/shard_map/while/body/eval_jaxpr/skc,cd->skd/dot_general | solution.py:66
  30.4 1.9 %fusion.287 = f32[64,32,256]{2,1,0:T(8,128)S(1)} fusion(f32[64,32,128]{2,1,0:T(8,128)S(1)} %get-tuple-element.514, f32[64,32,128]{2,1,0:T(8,128)S(1)} %get-tuple-element.515, f32[256,256]{1,0:T(8,128)S(1)} %get-tuple-element.544), kind=kOutput, calls=%fused_computation.5.clone.1 | convolution fusion | flops 1611137024 | bytes 4456448 | tf_op jit(solution)/shard_map/while/body/eval_jaxpr/skc,cd->skd/dot_general | solution.py:66
  38.9 2.0 %fusion.285 = f32[64,32,256]{2,1,0:T(8,128)S(1)} fusion(f32[64,16,256]{2,1,0:T(8,128)S(1)} %bitcast.89, f32[64,16,256]{2,1,0:T(8,128)S(1)} %bitcast.87), kind=kOutput, calls=%fused_computation.16.clone.1 | convolution fusion | flops 201865216 | bytes 4194304 | tf_op jit(solution)/shard_map/while/body/eval_jaxpr/kn,snc->skc/dot_general | solution.py:55
  40.9 2.0 %fusion.284 = f32[64,32,256]{2,1,0:T(8,128)S(1)} fusion(f32[64,16,256]{2,1,0:T(8,128)S(1)} %bitcast.90, f32[64,16,256]{2,1,0:T(8,128)S(1)} %bitcast.88), kind=kOutput, calls=%fused_computation.17.clone.1 | convolution fusion | flops 201865216 | bytes 4194304 | tf_op jit(solution)/shard_map/while/body/eval_jaxpr/kn,snc->skc/dot_general | solution.py:56
  45.8 1.9 %fusion.286 = f32[64,32,256]{2,1,0:T(8,128)S(1)} fusion(f32[64,32,128]{2,1,0:T(8,128)S(1)} %get-tuple-element.512, f32[64,32,128]{2,1,0:T(8,128)S(1)} %get-tuple-element.513, f32[256,256]{1,0:T(8,128)S(1)} %get-tuple-element.544), kind=kOutput, calls=%fused_computation.10.clone.1 | convolution fusion | flops 1611137024 | bytes 4456448 | tf_op jit(solution)/shard_map/while/body/eval_jaxpr/skc,cd->skd/dot_general | solution.py:66
  47.7 1.9 %fusion.287 = f32[64,32,256]{2,1,0:T(8,128)S(1)} fusion(f32[64,32,128]{2,1,0:T(8,128)S(1)} %get-tuple-element.514, f32[64,32,128]{2,1,0:T(8,128)S(1)} %get-tuple-element.515, f32[256,256]{1,0:T(8,128)S(1)} %get-tuple-element.544), kind=kOutput, calls=%fused_computation.5.clone.1 | convolution fusion | flops 1611137024 | bytes 4456448 | tf_op jit(solution)/shard_map/while/body/eval_jaxpr/skc,cd->skd/dot_general | solution.py:66
  56.1 2.0 %fusion.285 = f32[64,32,256]{2,1,0:T(8,128)S(1)} fusion(f32[64,16,256]{2,1,0:T(8,128)S(1)} %bitcast.89, f32[64,16,256]{2,1,0:T(8,128)S(1)} %bitcast.87), kind=kOutput, calls=%fused_computation.16.clone.1 | convolution fusion | flops 201865216 | bytes 4194304 | tf_op jit(solution)/shard_map/while/body/eval_jaxpr/kn,snc->skc/dot_general | solution.py:55
  58.1 2.0 %fusion.284 = f32[64,32,256]{2,1,0:T(8,128)S(1)} fusion(f32[64,16,256]{2,1,0:T(8,128)S(1)} %bitcast.90, f32[64,16,256]{2,1,0:T(8,128)S(1)} %bitcast.88), kind=kOutput, calls=%fused_computation.17.clone.1 | convolution fusion | flops 201865216 | bytes 4194304 | tf_op jit(solution)/shard_map/while/body/eval_jaxpr/kn,snc->skc/dot_general | solution.py:56
  63.0 1.9 %fusion.286 = f32[64,32,256]{2,1,0:T(8,128)S(1)} fusion(f32[64,32,128]{2,1,0:T(8,128)S(1)} %get-tuple-element.512, f32[64,32,128]{2,1,0:T(8,128)S(1)} %get-tuple-element.513, f32[256,256]{1,0:T(8,128)S(1)} %get-tuple-element.544), kind=kOutput, calls=%fused_computation.10.clone.1 | convolution fusion | flops 1611137024 | bytes 4456448 | tf_op jit(solution)/shard_map/while/body/eval_jaxpr/skc,cd->skd/dot_general | solution.py:66
  64.9 1.9 %fusion.287 = f32[64,32,256]{2,1,0:T(8,128)S(1)} fusion(f32[64,32,128]{2,1,0:T(8,128)S(1)} %get-tuple-element.514, f32[64,32,128]{2,1,0:T(8,128)S(1)} %get-tuple-element.515, f32[256,256]{1,0:T(8,128)S(1)} %get-tuple-element.544), kind=kOutput, calls=%fused_computation.5.clone.1 | convolution fusion | flops 1611137024 | bytes 4456448 | tf_op jit(solution)/shard_map/while/body/eval_jaxpr/skc,cd->skd/dot_general | solution.py:66
  71.0 3.8 %reshape.198 = f32[8,1,2048]{2,1,0:T(1,128)} reshape(f32[2048,2,4]{2,1,0:T(2,128)S(1)} %bitcast.93) | data formatting | bytes 131072
  74.8 7.3 %all-to-all-start = ((f32[8,1,2048]{2,1,0:T(1,128)}), f32[8,1,2048]{2,1,0:T(1,128)S(1)}, u32[]{:S(2)}, u32[]{:S(2)}) async-start(f32[8,1,2048]{2,1,0:T(1,128)} %reshape.198), calls=%async_computation | async-start | bytes 131072 | tf_op jit(solution)/shard_map/all_to_all | solution.py:150
  83.7 11.9 %all-reduce.1 = s32[32]{0:T(128)S(1)} all-reduce(s32[32]{0:T(128)S(1)} %dynamic-update-slice), channel_id=1, replica_groups=mesh['tm'=8,'chan'=4] {'tm'}, use_global_device_ids=true, to_apply=%add.1 | all-reduce | flops 32 | bytes 256
  97.6 3.2 %reshape.199 = f32[2048,2,4]{2,1,0:T(2,128)S(1)} reshape(f32[8,2048]{1,0:T(8,128)S(1)} %reduce.1) | data formatting | bytes 131072
  110.6 3.4 %collective-permute-start = (f32[24,512]{1,0:T(8,128)S(1)}, f32[24,512]{1,0:T(8,128)S(1)}, u32[]{:S(2)}, u32[]{:S(2)}) collective-permute-start(f32[24,512]{1,0:T(8,128)S(1)} %get-tuple-element.415), channel_id=1, source_target_pairs={{0,4},{4,8},{8,12},{12,16},{16,20},{20,24},{24,28},{1,5},{5,9},{9,... | collective-permute-start | bytes 147464 | tf_op jit(solution)/shard_map/ppermute | solution.py:22
  115.7 4.3 %collective-permute-done.1 = f32[24,512]{1,0:T(8,128)S(1)} collective-permute-done((f32[24,512]{1,0:T(8,128)S(1)}, f32[24,512]{1,0:T(8,128)S(1)}, u32[]{:S(2)}, u32[]{:S(2)}) %collective-permute-start.1) | collective-permute-done | bytes 49184 | tf_op jit(solution)/shard_map/ppermute | solution.py:23
  120.0 6.7 %fusion.100 = f32[256,512]{1,0:T(8,128)} fusion(f32[24,512]{1,0:T(8,128)S(1)} %collective-permute-done.1, f32[256,512]{1,0:T(8,128)S(1)} %fusion.106, f32[24,512]{1,0:T(8,128)S(1)} %collective-permute-done, f32[256,1]{1,0:T(8,128)S(1)} %get-tuple-element.412, f32[256,511]{1,0:T(8,128)S(1)} %get-tuple-element.414, f32[256,511]{1,0:T(8,128)S(1)} %get-tuple-element.413, ...), kind=kOutput, calls=%fused_computation.128 | convolution fusion | flops 495104000 | bytes 26342592 | tf_op jit(solution)/shard_map/dot_general | solution.py:172
  (164 shorter events, 53.4 us)
Async XLA Ops:
  69.6 12.4 %copy-start.3 = (u32[32]{0:T(128)S(1)}, u32[32]{0:T(128)}, u32[]{:S(2)}) copy-start(u32[32]{0:T(128)} %constant.235) | copy-start | bytes 388
  69.7 13.8 %copy-start.2 = (s32[4]{0:T(128)S(1)}, s32[4]{0:T(128)}, u32[]{:S(2)}) copy-start(s32[4]{0:T(128)} %param.10) | copy-start | bytes 52
  69.7 25.9 %copy-start = (s32[256]{0:T(256)S(1)}, s32[256]{0:T(256)}, u32[]{:S(2)}) copy-start(s32[256]{0:T(256)} %param.12) | copy-start | bytes 3076
  69.7 25.9 %copy-start.1 = (s32[256]{0:T(256)S(1)}, s32[256]{0:T(256)}, u32[]{:S(2)}) copy-start(s32[256]{0:T(256)} %param.13) | copy-start | bytes 3076
  74.8 21.5 %all-to-all-start = ((f32[8,1,2048]{2,1,0:T(1,128)}), f32[8,1,2048]{2,1,0:T(1,128)S(1)}, u32[]{:S(2)}, u32[]{:S(2)}) async-start(f32[8,1,2048]{2,1,0:T(1,128)} %reshape.198), calls=%async_computation | async-start | bytes 131072 | tf_op jit(solution)/shard_map/all_to_all | solution.py:150
  110.6 5.1 %collective-permute-start = (f32[24,512]{1,0:T(8,128)S(1)}, f32[24,512]{1,0:T(8,128)S(1)}, u32[]{:S(2)}, u32[]{:S(2)}) collective-permute-start(f32[24,512]{1,0:T(8,128)S(1)} %get-tuple-element.415), channel_id=1, source_target_pairs={{0,4},{4,8},{8,12},{12,16},{16,20},{20,24},{24,28},{1,5},{5,9},{9,... | collective-permute-start | bytes 147464 | tf_op jit(solution)/shard_map/ppermute | solution.py:22
  114.0 6.0 %collective-permute-start.1 = (f32[24,512]{1,0:T(8,128)S(1)}, f32[24,512]{1,0:T(8,128)S(1)}, u32[]{:S(2)}, u32[]{:S(2)}) collective-permute-start(f32[24,512]{1,0:T(8,128)S(1)} %get-tuple-element.416), channel_id=1, source_target_pairs={{4,0},{8,4},{12,8},{16,12},{20,16},{24,20},{28,24},{5,1},{9,5},{13... | collective-permute-start | bytes 147464 | tf_op jit(solution)/shard_map/ppermute | solution.py:23
where the time goes:
time: 127 us
  matrix products  50.9 us (40%)
  local copies, waits for them, and re-layouts  28.4 us (22%)
  other arithmetic  17.3 us (14%)
  starting transfers between devices  12.2 us (10%)
  blocking collectives  11.9 us (9%)
  waiting for transfers between devices  4.46 us (4%)
    dot_general x8, matrix products, forward(): return jnp.einsum('skc,cd->skd', turned, mixer, precision=HIGH)  15.2 us
    dot_general x8, matrix products, forward(): second = jnp.einsum('kn,snc->skc', small_sin, signal, precision=HIGH)  12.2 us
    dot_general x8, matrix products, forward(): first = jnp.einsum('kn,snc->skc', small_cos, signal, precision=HIGH)  12.2 us
    unnamed x1, blocking collectives  11.9 us
    dynamic_slice x8, local copies, waits for them, and re-layouts, body(): lax.map(lambda item: correlate(item[0], item[1], item[2], tables), (surve...  9.53 us
    unnamed x15, local copies, waits for them, and re-layouts  7.96 us
    slice x48, local copies, waits for them, and re-layouts, body(): jnp.roll(power, step, axis=1)  7.45 us
    all_to_all x1, starting transfers between devices, body(): lax.all_to_all(jnp.stack([real_c, imag_c], axis=1), 'tm', split_axis=2, c...  7.27 us
  transfers between devices with their start and end apart: 3, of which 2 were waited for; matrix products, arithmetic and copies ran while one was open for 1% of the time, Pallas kernels for 0%

commit v1 on v0

--- a/solution.py
+++ b/solution.py
@@ -147,9 +147,11 @@
     real_c = corr[:, :, :128].reshape(blocks, D)
     imag_c = corr[:, :, 128:].reshape(blocks, D)
     norm = 1.0 / math.sqrt(total_blocks * SEGS * D)
-    moved = lax.all_to_all(
-        jnp.stack([real_c, imag_c], axis=1), "tm", split_axis=2, concat_axis=0, tiled=True
-    )
+    value = jnp.stack([real_c, imag_c], axis=1)
+    peers = lax.axis_size("tm")
+    pieces = jnp.stack(jnp.split(value, peers, axis=2), axis=0)
+    pieces = lax.all_to_all(pieces, "tm", split_axis=0, concat_axis=0)
+    moved = jnp.concatenate(pieces, axis=0)
     ids = lax.all_gather(block_ids, "tm", axis=0, tiled=True)
     stacked = jnp.concatenate([moved[:, 0], moved[:, 1]], 0)
     mixer = doppler_mixer(ids, norm)

time: 127 us -> 122 us (0.961)
  local copies, waits for them, and re-layouts: 28.4 us -> 18.7 us
  other arithmetic: 17.3 us -> 21.4 us
    unnamed x15 -> x13, local copies, waits for them, and re-layouts: 7.96 us -> 0.93 us
    unnamed x0 -> x7, other arithmetic: none -> 4.26 us
    all_to_all x3 -> x0, local copies, waits for them, and re-layouts: 1.39 us -> none  [body(): lax.all_to_all(jnp.stack([real_c, imag_c], axis=1), 'tm', split_axis=2, c...]
    another operation x3 -> x0, local copies, waits for them, and re-layouts: 1.32 us -> none  [body(): jnp.stack([real_c, imag_c], axis=1)]
where the time goes in v1:
time: 122 us; the launch traced here: 121 us
  matrix products  50.9 us (42%)
  other arithmetic  21.4 us (18%)
  local copies, waits for them, and re-layouts  18.7 us (15%)
  starting transfers between devices  12.2 us (10%)
  blocking collectives  11.9 us (10%)
  waiting for transfers between devices  4.4 us (4%)
    dot_general x8, matrix products, forward(): return jnp.einsum('skc,cd->skd', turned, mixer, precision=HIGH)  15.2 us
    dot_general x8, matrix products, forward(): second = jnp.einsum('kn,snc->skc', small_sin, signal, precision=HIGH)  12.2 us
    dot_general x8, matrix products, forward(): first = jnp.einsum('kn,snc->skc', small_cos, signal, precision=HIGH)  12.2 us
    unnamed x1, blocking collectives  11.9 us
    dynamic_slice x8, local copies, waits for them, and re-layouts, body(): lax.map(lambda item: correlate(item[0], item[1], item[2], tables), (surve...  9.54 us
    slice x48, local copies, waits for them, and re-layouts, body(): jnp.roll(power, step, axis=1)  7.45 us
    all_to_all x1, starting transfers between devices, body(): pieces = lax.all_to_all(pieces, 'tm', split_axis=0, concat_axis=0)  7.29 us
    dot_general x1, matrix products, body(): delay_sum = jnp.dot(band, padded, precision=HIGH)  6.73 us
  transfers between devices with their start and end apart: 3, of which 2 were waited for; matrix products, arithmetic and copies ran while one was open for 1% of the time, Pallas kernels for 0%

profile of v1, /device:TPU:0, one launch (start us, length us, event | category | flops | bytes accessed | tf_op | source)
XLA Modules:
  0.0 121.0 jit_solution(17058484985489234353)
XLA Ops:
  0.6 69.0 %while.15 = (s32[]{:T(128)}, f32[4,16,256]{2,1,0:T(8,128)S(1)}, s32[4]{0:T(128)}, bf16[4,1024,256]{2,1,0:T(8,128)(2,1)}, f32[256,256]{1,0:T(8,128)S(1)}, /*index...) while((s32[]{:T(128)}, f32[4,16,256]{2,1,0:T(8,128)S(1)}, s32[4]{0:T(128)}, ...), condition=%wide.region_3.4_spmd.clone.clone, body=%wide.region_0.3_spmd.clone.clone.sunk | while | flops 4067001856 | bytes 47000764 | solution.py:144
  0.6 1.3 %dynamic_slice.37 = s32[1]{0:T(128)} dynamic-slice(s32[4]{0:T(128)} %get-tuple-element.542, s32[]{:T(128)S(6)} %copy.21), dynamic_slice_sizes={1} | dynamic-slice | bytes 12 | tf_op jit(solution)/shard_map/while/body/jit(dynamic_index_in_dim)/dynamic_slice | solution.py:144
  4.4 2.0 %fusion.293 = f32[64,32,256]{2,1,0:T(8,128)S(1)} fusion(f32[64,16,256]{2,1,0:T(8,128)S(1)} %bitcast.104, f32[64,16,256]{2,1,0:T(8,128)S(1)} %bitcast.102), kind=kOutput, calls=%fused_computation.16.clone.1 | convolution fusion | flops 201865216 | bytes 4194304 | tf_op jit(solution)/shard_map/while/body/eval_jaxpr/kn,snc->skc/dot_general | solution.py:55
  6.4 2.0 %fusion.292 = f32[64,32,256]{2,1,0:T(8,128)S(1)} fusion(f32[64,16,256]{2,1,0:T(8,128)S(1)} %bitcast.105, f32[64,16,256]{2,1,0:T(8,128)S(1)} %bitcast.103), kind=kOutput, calls=%fused_computation.17.clone.1 | convolution fusion | flops 201865216 | bytes 4194304 | tf_op jit(solution)/shard_map/while/body/eval_jaxpr/kn,snc->skc/dot_general | solution.py:56
  11.3 1.9 %fusion.294 = f32[64,32,256]{2,1,0:T(8,128)S(1)} fusion(f32[64,32,128]{2,1,0:T(8,128)S(1)} %get-tuple-element.512, f32[64,32,128]{2,1,0:T(8,128)S(1)} %get-tuple-element.513, f32[256,256]{1,0:T(8,128)S(1)} %get-tuple-element.544), kind=kOutput, calls=%fused_computation.10.clone.1 | convolution fusion | flops 1611137024 | bytes 4456448 | tf_op jit(solution)/shard_map/while/body/eval_jaxpr/skc,cd->skd/dot_general | solution.py:66
  13.2 1.9 %fusion.295 = f32[64,32,256]{2,1,0:T(8,128)S(1)} fusion(f32[64,32,128]{2,1,0:T(8,128)S(1)} %get-tuple-element.514, f32[64,32,128]{2,1,0:T(8,128)S(1)} %get-tuple-element.515, f32[256,256]{1,0:T(8,128)S(1)} %get-tuple-element.544), kind=kOutput, calls=%fused_computation.5.clone.1 | convolution fusion | flops 1611137024 | bytes 4456448 | tf_op jit(solution)/shard_map/while/body/eval_jaxpr/skc,cd->skd/dot_general | solution.py:66
  21.7 2.0 %fusion.293 = f32[64,32,256]{2,1,0:T(8,128)S(1)} fusion(f32[64,16,256]{2,1,0:T(8,128)S(1)} %bitcast.104, f32[64,16,256]{2,1,0:T(8,128)S(1)} %bitcast.102), kind=kOutput, calls=%fused_computation.16.clone.1 | convolution fusion | flops 201865216 | bytes 4194304 | tf_op jit(solution)/shard_map/while/body/eval_jaxpr/kn,snc->skc/dot_general | solution.py:55
  23.7 2.0 %fusion.292 = f32[64,32,256]{2,1,0:T(8,128)S(1)} fusion(f32[64,16,256]{2,1,0:T(8,128)S(1)} %bitcast.105, f32[64,16,256]{2,1,0:T(8,128)S(1)} %bitcast.103), kind=kOutput, calls=%fused_computation.17.clone.1 | convolution fusion | flops 201865216 | bytes 4194304 | tf_op jit(solution)/shard_map/while/body/eval_jaxpr/kn,snc->skc/dot_general | solution.py:56
  28.6 1.9 %fusion.294 = f32[64,32,256]{2,1,0:T(8,128)S(1)} fusion(f32[64,32,128]{2,1,0:T(8,128)S(1)} %get-tuple-element.512, f32[64,32,128]{2,1,0:T(8,128)S(1)} %get-tuple-element.513, f32[256,256]{1,0:T(8,128)S(1)} %get-tuple-element.544), kind=kOutput, calls=%fused_computation.10.clone.1 | convolution fusion | flops 1611137024 | bytes 4456448 | tf_op jit(solution)/shard_map/while/body/eval_jaxpr/skc,cd->skd/dot_general | solution.py:66
  30.5 1.9 %fusion.295 = f32[64,32,256]{2,1,0:T(8,128)S(1)} fusion(f32[64,32,128]{2,1,0:T(8,128)S(1)} %get-tuple-element.514, f32[64,32,128]{2,1,0:T(8,128)S(1)} %get-tuple-element.515, f32[256,256]{1,0:T(8,128)S(1)} %get-tuple-element.544), kind=kOutput, calls=%fused_computation.5.clone.1 | convolution fusion | flops 1611137024 | bytes 4456448 | tf_op jit(solution)/shard_map/while/body/eval_jaxpr/skc,cd->skd/dot_general | solution.py:66
  38.9 2.0 %fusion.293 = f32[64,32,256]{2,1,0:T(8,128)S(1)} fusion(f32[64,16,256]{2,1,0:T(8,128)S(1)} %bitcast.104, f32[64,16,256]{2,1,0:T(8,128)S(1)} %bitcast.102), kind=kOutput, calls=%fused_computation.16.clone.1 | convolution fusion | flops 201865216 | bytes 4194304 | tf_op jit(solution)/shard_map/while/body/eval_jaxpr/kn,snc->skc/dot_general | solution.py:55
  40.9 2.0 %fusion.292 = f32[64,32,256]{2,1,0:T(8,128)S(1)} fusion(f32[64,16,256]{2,1,0:T(8,128)S(1)} %bitcast.105, f32[64,16,256]{2,1,0:T(8,128)S(1)} %bitcast.103), kind=kOutput, calls=%fused_computation.17.clone.1 | convolution fusion | flops 201865216 | bytes 4194304 | tf_op jit(solution)/shard_map/while/body/eval_jaxpr/kn,snc->skc/dot_general | solution.py:56
  45.8 1.9 %fusion.294 = f32[64,32,256]{2,1,0:T(8,128)S(1)} fusion(f32[64,32,128]{2,1,0:T(8,128)S(1)} %get-tuple-element.512, f32[64,32,128]{2,1,0:T(8,128)S(1)} %get-tuple-element.513, f32[256,256]{1,0:T(8,128)S(1)} %get-tuple-element.544), kind=kOutput, calls=%fused_computation.10.clone.1 | convolution fusion | flops 1611137024 | bytes 4456448 | tf_op jit(solution)/shard_map/while/body/eval_jaxpr/skc,cd->skd/dot_general | solution.py:66
  47.7 1.9 %fusion.295 = f32[64,32,256]{2,1,0:T(8,128)S(1)} fusion(f32[64,32,128]{2,1,0:T(8,128)S(1)} %get-tuple-element.514, f32[64,32,128]{2,1,0:T(8,128)S(1)} %get-tuple-element.515, f32[256,256]{1,0:T(8,128)S(1)} %get-tuple-element.544), kind=kOutput, calls=%fused_computation.5.clone.1 | convolution fusion | flops 1611137024 | bytes 4456448 | tf_op jit(solution)/shard_map/while/body/eval_jaxpr/skc,cd->skd/dot_general | solution.py:66
  56.2 2.0 %fusion.293 = f32[64,32,256]{2,1,0:T(8,128)S(1)} fusion(f32[64,16,256]{2,1,0:T(8,128)S(1)} %bitcast.104, f32[64,16,256]{2,1,0:T(8,128)S(1)} %bitcast.102), kind=kOutput, calls=%fused_computation.16.clone.1 | convolution fusion | flops 201865216 | bytes 4194304 | tf_op jit(solution)/shard_map/while/body/eval_jaxpr/kn,snc->skc/dot_general | solution.py:55
  58.2 2.0 %fusion.292 = f32[64,32,256]{2,1,0:T(8,128)S(1)} fusion(f32[64,16,256]{2,1,0:T(8,128)S(1)} %bitcast.105, f32[64,16,256]{2,1,0:T(8,128)S(1)} %bitcast.103), kind=kOutput, calls=%fused_computation.17.clone.1 | convolution fusion | flops 201865216 | bytes 4194304 | tf_op jit(solution)/shard_map/while/body/eval_jaxpr/kn,snc->skc/dot_general | solution.py:56
  63.1 1.9 %fusion.294 = f32[64,32,256]{2,1,0:T(8,128)S(1)} fusion(f32[64,32,128]{2,1,0:T(8,128)S(1)} %get-tuple-element.512, f32[64,32,128]{2,1,0:T(8,128)S(1)} %get-tuple-element.513, f32[256,256]{1,0:T(8,128)S(1)} %get-tuple-element.544), kind=kOutput, calls=%fused_computation.10.clone.1 | convolution fusion | flops 1611137024 | bytes 4456448 | tf_op jit(solution)/shard_map/while/body/eval_jaxpr/skc,cd->skd/dot_general | solution.py:66
  65.0 1.9 %fusion.295 = f32[64,32,256]{2,1,0:T(8,128)S(1)} fusion(f32[64,32,128]{2,1,0:T(8,128)S(1)} %get-tuple-element.514, f32[64,32,128]{2,1,0:T(8,128)S(1)} %get-tuple-element.515, f32[256,256]{1,0:T(8,128)S(1)} %get-tuple-element.544), kind=kOutput, calls=%fused_computation.5.clone.1 | convolution fusion | flops 1611137024 | bytes 4456448 | tf_op jit(solution)/shard_map/while/body/eval_jaxpr/skc,cd->skd/dot_general | solution.py:66
  74.5 7.3 %all-to-all-start = ((f32[8,4,2,256]{3,2,1,0:T(2,128)}), f32[8,4,2,256]{3,2,1,0:T(2,128)S(1)}, u32[]{:S(2)}, u32[]{:S(2)}) async-start(f32[8,4,2,256]{3,2,1,0:T(2,128)} %constant_dynamic-update-slice_fusion), calls=%async_computation | async-start | bytes 131072 | tf_op jit(solution)/shard_map/all_to_all | solution.py:153
  83.4 11.9 %all-reduce.1 = s32[32]{0:T(128)S(1)} all-reduce(s32[32]{0:T(128)S(1)} %dynamic-update-slice), channel_id=1, replica_groups=mesh['tm'=8,'chan'=4] {'tm'}, use_global_device_ids=true, to_apply=%add.1 | all-reduce | flops 32 | bytes 256
  104.9 3.4 %collective-permute-start = (f32[24,512]{1,0:T(8,128)S(1)}, f32[24,512]{1,0:T(8,128)S(1)}, u32[]{:S(2)}, u32[]{:S(2)}) collective-permute-start(f32[24,512]{1,0:T(8,128)S(1)} %get-tuple-element.415), channel_id=1, source_target_pairs={{0,4},{4,8},{8,12},{12,16},{16,20},{20,24},{24,28},{1,5},{5,9},{9,... | collective-permute-start | bytes 147464 | tf_op jit(solution)/shard_map/ppermute | solution.py:22
  108.3 1.5 %collective-permute-start.1 = (f32[24,512]{1,0:T(8,128)S(1)}, f32[24,512]{1,0:T(8,128)S(1)}, u32[]{:S(2)}, u32[]{:S(2)}) collective-permute-start(f32[24,512]{1,0:T(8,128)S(1)} %get-tuple-element.416), channel_id=1, source_target_pairs={{4,0},{8,4},{12,8},{16,12},{20,16},{24,20},{28,24},{5,1},{9,5},{13... | collective-permute-start | bytes 147464 | tf_op jit(solution)/shard_map/ppermute | solution.py:23
  110.0 4.3 %collective-permute-done.1 = f32[24,512]{1,0:T(8,128)S(1)} collective-permute-done((f32[24,512]{1,0:T(8,128)S(1)}, f32[24,512]{1,0:T(8,128)S(1)}, u32[]{:S(2)}, u32[]{:S(2)}) %collective-permute-start.1) | collective-permute-done | bytes 49184 | tf_op jit(solution)/shard_map/ppermute | solution.py:23
  114.2 6.7 %fusion.100 = f32[256,512]{1,0:T(8,128)} fusion(f32[24,512]{1,0:T(8,128)S(1)} %collective-permute-done.1, f32[256,512]{1,0:T(8,128)S(1)} %fusion.106, f32[24,512]{1,0:T(8,128)S(1)} %collective-permute-done, f32[256,1]{1,0:T(8,128)S(1)} %get-tuple-element.412, f32[256,511]{1,0:T(8,128)S(1)} %get-tuple-element.414, f32[256,511]{1,0:T(8,128)S(1)} %get-tuple-element.413, ...), kind=kOutput, calls=%fused_computation.128 | convolution fusion | flops 495104000 | bytes 26342592 | tf_op jit(solution)/shard_map/dot_general | solution.py:174
  (162 shorter events, 51.9 us)
Async XLA Ops:
  0.6 81.2 %copy-start.3 = (u32[32]{0:T(128)S(1)}, u32[32]{0:T(128)}, u32[]{:S(2)}) copy-start(u32[32]{0:T(128)} %constant.235) | copy-start | bytes 388
  0.6 82.6 %copy-start.2 = (s32[4]{0:T(128)S(1)}, s32[4]{0:T(128)}, u32[]{:S(2)}) copy-start(s32[4]{0:T(128)} %param.10) | copy-start | bytes 52
  0.6 94.7 %copy-start = (s32[256]{0:T(256)S(1)}, s32[256]{0:T(256)}, u32[]{:S(2)}) copy-start(s32[256]{0:T(256)} %param.12) | copy-start | bytes 3076
  0.6 94.7 %copy-start.1 = (s32[256]{0:T(256)S(1)}, s32[256]{0:T(256)}, u32[]{:S(2)}) copy-start(s32[256]{0:T(256)} %param.13) | copy-start | bytes 3076
  74.5 21.5 %all-to-all-start = ((f32[8,4,2,256]{3,2,1,0:T(2,128)}), f32[8,4,2,256]{3,2,1,0:T(2,128)S(1)}, u32[]{:S(2)}, u32[]{:S(2)}) async-start(f32[8,4,2,256]{3,2,1,0:T(2,128)} %constant_dynamic-update-slice_fusion), calls=%async_computation | async-start | bytes 131072 | tf_op jit(solution)/shard_map/all_to_all | solution.py:153
  104.9 5.1 %collective-permute-start = (f32[24,512]{1,0:T(8,128)S(1)}, f32[24,512]{1,0:T(8,128)S(1)}, u32[]{:S(2)}, u32[]{:S(2)}) collective-permute-start(f32[24,512]{1,0:T(8,128)S(1)} %get-tuple-element.415), channel_id=1, source_target_pairs={{0,4},{4,8},{8,12},{12,16},{16,20},{20,24},{24,28},{1,5},{5,9},{9,... | collective-permute-start | bytes 147464 | tf_op jit(solution)/shard_map/ppermute | solution.py:22
  108.3 6.0 %collective-permute-start.1 = (f32[24,512]{1,0:T(8,128)S(1)}, f32[24,512]{1,0:T(8,128)S(1)}, u32[]{:S(2)}, u32[]{:S(2)}) collective-permute-start(f32[24,512]{1,0:T(8,128)S(1)} %get-tuple-element.416), channel_id=1, source_target_pairs={{4,0},{8,4},{12,8},{16,12},{20,16},{24,20},{28,24},{5,1},{9,5},{13... | collective-permute-start | bytes 147464 | tf_op jit(solution)/shard_map/ppermute | solution.py:23
